TPU v7x, 256 devices: a whole 4x4x8 slice. The times are simulated.
256 devices in a mesh: blk: 128 (over z_lo, y, x, core), rep: 2 (over z_hi).
Axes of the slice: x: 4, y: 4, z: 8 (z_hi: 2, z_lo: 4; z = z_hi * 4 + z_lo), core: 2. Of those that a mesh axis runs over, the one named last changes fastest.
Arguments:
- load_coef: bfloat16 [256, 2049, 256], P('blk', None, 'rep'), parts along dimension 2, may hold values from -0.29882812 to 0.29882812
- legendre: bfloat16 [256, 2049, 1024], P('blk'), may hold values from -0.125 to 0.125
- slab_orders: int32 [256], replicated, may hold values from 0 to 1023, as said below
- cycle_rows: int32 [1024], replicated, may hold values from 0 to 1023, each once
Outputs:
- potential: bfloat16 [1024, 128, 4096], P('blk', 'rep'), parts along dimension 1
- energy: float32 [128], P('rep'), parts along dimension 0
There are 2 independent parts, one for each index of `rep`. A program takes and returns all parts, laid end to end along the dimension named above; an argument that names none is the same for every part. Nothing has to cross between parts.
Inputs may be any that keep to these rules, and one draw needn't show every extreme that they name: `slab_orders`: values are distinct and below (2048) / 2. `cycle_rows`: each cycle appears once.
All inputs are finite; a program needn't handle non-finite values.
Results may differ from a plain program's by a relative error of at most 0.0055.
Values may be sent and summed in bfloat16 or wider, within the bound.
A program may use at most 128 MiB of HBM per device.

v0:
```python
import math

import jax
import jax.numpy as jnp
from jax import lax
from jax.experimental import pallas as pl
from jax.experimental.pallas import tpu as pltpu
from jax.sharding import PartitionSpec as P

BF16 = jnp.bfloat16
F32 = jnp.float32
I32 = jnp.int32
MESH = pl.DeviceIdType.MESH
NLON = 4096
HALF = NLON // 2
DEGREE = 2047
ROWS = 2049
NLAT = 1024
FIELDS = 64
NBLK = 128
PLANE = 32
COLS = 512


def sincos(phase):
    turned = (phase + 512) & 4095
    quadrant = turned >> 10
    theta = ((turned & 1023) - 512).astype(F32) * (2.0 * math.pi / NLON)
    t2 = theta * theta
    s = theta * (1.0 + t2 * (-1.0 / 6 + t2 * (1.0 / 120 + t2 * (-1.0 / 5040 + t2 * (1.0 / 362880)))))
    c = 1.0 + t2 * (-0.5 + t2 * (1.0 / 24 + t2 * (-1.0 / 720 + t2 * (1.0 / 40320))))
    odd = (quadrant & 1) == 1
    cosine = jnp.where(odd, s, c)
    sine = jnp.where(odd, c, s)
    flip_cos = ((quadrant + 1) & 2) == 2
    flip_sin = (quadrant & 2) == 2
    return jnp.where(flip_cos, -cosine, cosine), jnp.where(flip_sin, -sine, sine)


def exchange(
    orders_hbm, cycles_hbm, coef_hbm, leg_hbm,
    even_x, odd_x, basis, energy_ref,
    orders_v, cycles, coef, leg, stacked, spec, onehot, outbox, inbox, wide, order_cols, e_mine, e_plane, e_all,
    small_sems, coef_sem, leg_sem, send_sem, recv_sem, e_sems, ring_sems,
):
    me = lax.axis_index("blk")
    z, y, x, c = me // 32, (me // 8) % 4, (me // 2) % 4, me % 2

    def at(dz, dy, dx, dc):
        return (((z + dz) % 4 * 4 + (y + dy) % 4) * 4 + (x + dx) % 4) * 2 + (c + dc) % 2

    near = [(d, 0, 0, 0) for d in (1, 2, 3)] + [(0, d, 0, 0) for d in (1, 2, 3)]
    near += [(0, 0, d, 0) for d in (1, 2, 3)] + [(0, 0, 0, 1)]

    orders_copy = pltpu.make_async_copy(orders_hbm, orders_v, small_sems.at[0])
    orders_copy.start()
    cycles_copy = pltpu.make_async_copy(cycles_hbm, cycles, small_sems.at[1])
    cycles_copy.start()
    coef_copy = pltpu.make_async_copy(coef_hbm, coef, coef_sem)
    coef_copy.start()
    leg_copies = [pltpu.make_async_copy(leg_hbm.at[:, jt], leg.at[jt], leg_sem.at[jt]) for jt in range(8)]
    for copy in leg_copies:
        copy.start()

    barrier = pltpu.get_barrier_semaphore()

    def signal(sem):
        for offset in near:
            pl.semaphore_signal(sem, inc=1, device_id={"blk": at(*offset)}, device_id_type=MESH)

    signal(barrier)

    orders_copy.wait()
    for h in range(2):
        order_cols[h * 128 : (h + 1) * 128, :] = jnp.broadcast_to(orders_v[h : h + 1, :], (128, 128)).T
    cycles_copy.wait()
    lanes = lax.broadcasted_iota(I32, (128, 128), 1)
    for ib in range(8):
        wanted = jnp.broadcast_to(cycles[ib : ib + 1, :], (128, 128)).T
        for jb in range(8):
            onehot[ib * 128 : (ib + 1) * 128, jb * 128 : (jb + 1) * 128] = jnp.where(
                wanted == lanes + jb * 128, 1.0, 0.0
            ).astype(BF16)

    coef_copy.wait()
    packed = coef[...].reshape(2 * ROWS, 128).T
    column = lax.broadcasted_iota(I32, (1, 2 * ROWS), 1)
    row_id, pair_id = column >> 1, column & 1
    for p in range(2):
        order = order_cols[pl.ds(me * 2 + p, 1), :][:, :1]
        lower = jnp.where(row_id < DEGREE + 1 - order, 1, 0)
        parity_of = jnp.where(pair_id == p, (lower + order + 1) & 1, 2)
        for parity in range(2):
            keep = jnp.where(parity_of == parity, 1.0, 0.0).astype(BF16)
            for part in range(2):
                row = ((p * 2 + part) * 2 + parity) * 64
                stacked[row : row + 64, :] = packed[part * 64 : (part + 1) * 64] * keep

    pl.semaphore_wait(barrier, 10)
    signal(ring_sems.at[0])
    for jp in range(4):
        leg_copies[2 * jp].wait()
        leg_copies[2 * jp + 1].wait()
        table = jnp.concatenate(
            [leg[2 * jp].reshape(2 * ROWS, 128), leg[2 * jp + 1].reshape(2 * ROWS, 128)], axis=1
        )
        spec[:, jp * 256 : (jp + 1) * 256] = jnp.dot(
            stacked[...], table, preferred_element_type=F32
        ).astype(BF16)
        if jp == 2:
            pl.semaphore_wait(ring_sems.at[0], 10)
            signal(ring_sems.at[1])
    outbox[...] = (
        lax.dot_general(onehot[...], spec[...], (((1,), (1,)), ((), ())), preferred_element_type=F32)
        .reshape(NBLK, 8, COLS)
        .astype(BF16)
    )

    def send(dz, dy, dx, dc):
        target = at(dz, dy, dx, dc)
        pltpu.make_async_remote_copy(
            src_ref=outbox.at[target], dst_ref=inbox.at[me], send_sem=send_sem, recv_sem=recv_sem.at[dz],
            device_id={"blk": target}, device_id_type=MESH,
        ).start()

    def send_all(planes, axes, flip):
        count = 3 ** len(axes)

        def one(t, carry):
            offset = [0, 0, 0, flip]
            rest = t
            for axis in axes:
                offset[axis] = rest % 3 + 1
                rest = rest // 3
            for dz in planes:
                send(dz, *offset[1:])
            return carry

        if count == 1:
            one(0, 0)
        else:
            lax.fori_loop(0, count, one, 0)

    across = (2, 1, 3)
    send_all(across, (), 0)
    send_all((2, 1, 3, 0), (2,), 0)
    send_all((2, 1, 3, 0), (1,), 0)
    send_all((2, 1, 3, 0), (), 1)
    for axes, flip in (((1, 2), 0), ((1,), 1), ((2,), 1)):
        send_all((0,), axes, flip)
    pl.semaphore_wait(ring_sems.at[1], 10)
    signal(ring_sems.at[2])
    for axes, flip in (((1, 2), 0), ((1,), 1), ((2,), 1)):
        send_all((2,), axes, flip)
    send_all((0,), (1, 2), 1)
    pl.semaphore_wait(ring_sems.at[2], 10)
    send_all((2,), (1, 2), 1)
    for axes, flip in (((1, 2), 0), ((1,), 1), ((2,), 1), ((1, 2), 1)):
        send_all((1, 3), axes, flip)
    inbox[me] = outbox[me]

    place = me % PLANE
    is_even = lax.broadcasted_iota(I32, (1, 128), 1) < FIELDS
    energy = jnp.zeros((1, 128), F32)
    for p in range(2):
        order = order_cols[pl.ds(me * 2 + p, 1), :]
        has_zero = jnp.where(order % 2 == 1, DEGREE - order, order) == 0
        for part in range(2):
            row = (p * 2 + part) * 128
            squares = jnp.zeros((128, 128), F32)
            for jb in range(8):
                values = spec[row : row + 128, jb * 128 : (jb + 1) * 128].astype(F32)
                squares = squares + values * values
            weight = jnp.where(is_even, jnp.where(has_zero, 1.0 - part, 2.0), 2.0)
            energy = energy + weight * jnp.sum(squares.T, axis=0, keepdims=True)
    e_mine[0] = energy
    e_plane[place] = energy

    def tell(t, carry):
        target = at(0, t // 8, (t // 2) % 4, t % 2)
        pltpu.make_async_remote_copy(
            src_ref=e_mine.at[0], dst_ref=e_plane.at[place], send_sem=e_sems.at[0], recv_sem=e_sems.at[1],
            device_id={"blk": target}, device_id_type=MESH,
        ).start()
        return carry

    lax.fori_loop(1, PLANE, tell, 0)

    def basis_step(step, carry):
        a, part = step // 16, step % 16
        back, sub = part // 4, part % 4
        first = (z + 4 - back) % 4 * 64 + sub * 16
        col = pl.multiple_of(a * 128, 128)
        for p in range(2):
            order = order_cols[pl.ds(first + p, 8, stride=2), :]
            even = jnp.where((order & 1) == 1, DEGREE - order, order)
            k = lax.broadcasted_iota(I32, (8, 128), 1) + a * 128
            for parity in range(2):
                m = even if parity == 0 else DEGREE - even
                cosine, sine = sincos(m * k)
                factor = jnp.where(m == 0, 1.0, 2.0)
                row = pl.multiple_of(parity * COLS + back * 128 + p * 64 + sub * 8, 8)
                basis[pl.ds(row, 8), pl.ds(col, 128)] = (factor * cosine).astype(BF16)
                row = pl.multiple_of(parity * COLS + back * 128 + p * 64 + 32 + sub * 8, 8)
                basis[pl.ds(row, 8), pl.ds(col, 128)] = (-factor * sine).astype(BF16)
        return carry

    lax.fori_loop(0, 256, basis_step, 0)

    told = pltpu.make_async_remote_copy(
        src_ref=e_plane.at[pl.ds(0, PLANE - 1)], dst_ref=e_plane.at[pl.ds(0, PLANE - 1)],
        send_sem=e_sems.at[0], recv_sem=e_sems.at[1], device_id={"blk": at(0, 0, 0, 1)}, device_id_type=MESH,
    )
    told.wait_send()
    told.wait_recv()
    total = e_plane[0]
    for s in range(1, PLANE):
        total = total + e_plane[s]
    e_mine[1] = total
    e_all[z] = total
    for d in range(1, 4):
        pltpu.make_async_remote_copy(
            src_ref=e_mine.at[1], dst_ref=e_all.at[z], send_sem=e_sems.at[2], recv_sem=e_sems.at[3],
            device_id={"blk": at(d, 0, 0, 0)}, device_id_type=MESH,
        ).start()

    for back in (0, 2, 1, 3):
        plane = (z + 4 - back) % 4
        count = PLANE - 1 if back == 0 else PLANE
        come = pltpu.make_async_remote_copy(
            src_ref=outbox.at[pl.ds(0, count)], dst_ref=inbox.at[pl.ds(0, count)],
            send_sem=send_sem, recv_sem=recv_sem.at[back], device_id={"blk": at(0, 0, 0, 1)}, device_id_type=MESH,
        )
        come.wait_recv()
        for g in range(4):
            wide[g] = (
                inbox[pl.ds(plane * PLANE, PLANE), :, g * 128 : (g + 1) * 128].astype(F32).reshape(256, 128)
            )
        for i in range(8):
            block = jnp.concatenate([wide[g, pl.ds(i, PLANE, stride=8), :] for g in range(4)], axis=0)
            block = block.T.astype(BF16)
            even_x[i * 64 : (i + 1) * 64, back * 128 : (back + 1) * 128] = block[:64]
            odd_x[i * 64 : (i + 1) * 64, back * 128 : (back + 1) * 128] = block[64:]

    told = pltpu.make_async_remote_copy(
        src_ref=e_all.at[pl.ds(0, 3)], dst_ref=e_all.at[pl.ds(0, 3)],
        send_sem=e_sems.at[2], recv_sem=e_sems.at[3], device_id={"blk": at(0, 0, 0, 1)}, device_id_type=MESH,
    )
    told.wait_send()
    told.wait_recv()
    energy_ref[...] = (e_all[0] + e_all[1]) + (e_all[2] + e_all[3])
    sent = pltpu.make_async_remote_copy(
        src_ref=outbox.at[pl.ds(0, NBLK - 1)], dst_ref=inbox.at[pl.ds(0, NBLK - 1)],
        send_sem=send_sem, recv_sem=recv_sem.at[0], device_id={"blk": at(0, 0, 0, 1)}, device_id_type=MESH,
    )
    sent.wait_send()


def synthesize(energy_in, even_x, odd_x, basis, potential_hbm, energy_ref, tile, tile_sems):
    both = energy_in[...]
    energy_ref[...] = (both[:, :FIELDS] + both[:, FIELDS:]) * (1.0 / NLAT)
    steps = HALF // 256

    def out_copy(step, half):
        return pltpu.make_async_copy(
            tile.at[step, half],
            potential_hbm.at[:, :, pl.ds(half * HALF + step * 256, 256)],
            tile_sems.at[step, half],
        )

    for n in range(steps):
        evens = jnp.dot(even_x[...], basis[:COLS, n * 256 : (n + 1) * 256], preferred_element_type=F32)
        odds = jnp.dot(odd_x[...], basis[COLS:, n * 256 : (n + 1) * 256], preferred_element_type=F32)
        tile[n, 0] = (evens + odds).astype(BF16).reshape(8, FIELDS, 256)
        tile[n, 1] = (evens - odds).astype(BF16).reshape(8, FIELDS, 256)
        for half in range(2):
            out_copy(n, half).start()
    for n in range(steps):
        for half in range(2):
            out_copy(n, half).wait()


def shards(load_coef, legendre, slab_orders, cycle_rows):
    any_space = pl.BlockSpec(memory_space=pl.ANY)
    vmem = pl.BlockSpec(memory_space=pltpu.VMEM)
    coef = load_coef.transpose(1, 0, 2)
    table = legendre.transpose(1, 0, 2).reshape(ROWS, 2, 8, 128).transpose(0, 2, 1, 3)
    even_x, odd_x, basis, energy = pl.pallas_call(
        exchange,
        out_shape=(
            jax.ShapeDtypeStruct((COLS, COLS), BF16),
            jax.ShapeDtypeStruct((COLS, COLS), BF16),
            jax.ShapeDtypeStruct((2 * COLS, HALF), BF16),
            jax.ShapeDtypeStruct((1, 128), F32),
        ),
        in_specs=[pl.BlockSpec(memory_space=pltpu.HBM)] * 4,
        out_specs=(vmem, vmem, vmem, vmem),
        scratch_shapes=[
            pltpu.VMEM((2, 128), I32),
            pltpu.VMEM((8, 128), I32),
            pltpu.VMEM((ROWS, 2, 128), BF16),
            pltpu.VMEM((8, ROWS, 2, 128), BF16),
            pltpu.VMEM((COLS, 2 * ROWS), BF16),
            pltpu.VMEM((COLS, NLAT), BF16),
            pltpu.VMEM((NLAT, NLAT), BF16),
            pltpu.VMEM((NBLK, 8, COLS), BF16),
            pltpu.VMEM((NBLK, 8, COLS), BF16),
            pltpu.VMEM((4, 256, 128), F32),
            pltpu.VMEM((256, 128), I32),
            pltpu.VMEM((2, 1, 128), F32),
            pltpu.VMEM((PLANE, 1, 128), F32),
            pltpu.VMEM((4, 1, 128), F32),
            pltpu.SemaphoreType.DMA((2,)),
            pltpu.SemaphoreType.DMA,
            pltpu.SemaphoreType.DMA((8,)),
            pltpu.SemaphoreType.DMA,
            pltpu.SemaphoreType.DMA((4,)),
            pltpu.SemaphoreType.DMA((4,)),
            pltpu.SemaphoreType.REGULAR((3,)),
        ],
        compiler_params=pltpu.CompilerParams(
            collective_id=0, has_side_effects=True, vmem_limit_bytes=44 * 1024 * 1024
        ),
        name="exchange",
    )(*[pltpu.with_memory_space_constraint(a, pltpu.HBM) for a in (slab_orders.reshape(2, 128), cycle_rows.reshape(8, 128), coef, table)])
    potential, energy = pl.pallas_call(
        synthesize,
        out_shape=(
            jax.ShapeDtypeStruct((8, FIELDS, NLON), BF16),
            jax.ShapeDtypeStruct((1, FIELDS), F32),
        ),
        in_specs=[vmem, vmem, vmem, vmem],
        out_specs=(any_space, vmem),
        scratch_shapes=[
            pltpu.VMEM((8, 2, 8, FIELDS, 256), BF16),
            pltpu.SemaphoreType.DMA((8, 2)),
        ],
        compiler_params=pltpu.CompilerParams(vmem_limit_bytes=24 * 1024 * 1024),
        name="synthesize",
    )(energy, even_x, odd_x, basis)
    return potential, energy.reshape(FIELDS)


def solution(mesh):
    in_specs = (P("blk", None, "rep"), P("blk", None, None), P(), P())
    out_specs = (P("blk", "rep", None), P("rep"))
    return jax.shard_map(shards, mesh=mesh, in_specs=in_specs, out_specs=out_specs, check_vma=False)
```

profile of v0, /device:TPU:33, one launch (start us, length us, event | category | flops | bytes accessed | tf_op | source)
XLA Modules:
  0.0 50.7 jit_solution(10642742028584883638)
XLA Ops:
  0.6 46.1 %exchange.1 = (bf16[512,512]{1,0:T(8,128)(2,1)S(1)}, bf16[512,512]{1,0:T(8,128)(2,1)S(1)}, bf16[1024,2048]{1,0:T(8,128)(2,1)S(1)}, f32[1,128]{1,0:T(1,128)S(1)}) custom-call(s32[2,128]{1,0:T(2,128)} %bitcast.12, s32[8,128]{1,0:T(8,128)} %bitcast.11, bf16[2049,2,128]{2,1,0:T(2,128)(2,1)} %bitcast.10, bf16[2049,8,2,128]{3,2,1,0:T(2,128)(2,1)} %bitcast.9), custom_call_target="tpu_custom_call" | custom-call | tf_op jit(solution)/shard_map/exchange/pallas_call | solution.py:288
  46.7 3.8 %synthesize.1 = (bf16[8,64,4096]{2,1,0:T(8,128)(2,1)}, f32[1,64]{1,0:T(1,128)}) custom-call(f32[1,128]{1,0:T(1,128)S(1)} %get-tuple-element.8.energy_in, bf16[512,512]{1,0:T(8,128)(2,1)S(1)} %get-tuple-element.9.even_x, bf16[512,512]{1,0:T(8,128)(2,1)S(1)} %get-tuple-element.10.odd_x, bf16[1024,2048]{1,0:T(8,128)(2,1)S(1)} %get-tuple-element.11.basis), custom_call_target="tpu_custom_call" | custom-call | tf_op jit(solution)/shard_map/synthesize/pallas_call | solution.py:326
where the time goes:
time: 50.8 us; the launch traced here: 50.7 us
  Pallas kernels  49.9 us (98%)
  between operations  0.8 us (2%)
    pallas_call x1, Pallas kernels, shards(): pl.pallas_call(exchange, out_shape=(jax.ShapeDtypeStruct((COLS, COLS), BF...  46.1 us
    pallas_call x1, Pallas kernels, shards(): pl.pallas_call(synthesize, out_shape=(jax.ShapeDtypeStruct((8, FIELDS, NL...  3.81 us

commit v1 on v0

--- a/solution.py
+++ b/solution.py
@@ -59,8 +59,6 @@
     coef_copy = pltpu.make_async_copy(coef_hbm, coef, coef_sem)
     coef_copy.start()
     leg_copies = [pltpu.make_async_copy(leg_hbm.at[:, jt], leg.at[jt], leg_sem.at[jt]) for jt in range(8)]
-    for copy in leg_copies:
-        copy.start()
 
     barrier = pltpu.get_barrier_semaphore()
 
@@ -75,14 +73,21 @@
         order_cols[h * 128 : (h + 1) * 128, :] = jnp.broadcast_to(orders_v[h : h + 1, :], (128, 128)).T
     cycles_copy.wait()
     lanes = lax.broadcasted_iota(I32, (128, 128), 1)
-    for ib in range(8):
-        wanted = jnp.broadcast_to(cycles[ib : ib + 1, :], (128, 128)).T
+
+    def pick(ib, carry):
+        wanted = jnp.broadcast_to(cycles[pl.ds(ib, 1), :], (128, 128)).T
+        row = pl.multiple_of(ib * 128, 128)
         for jb in range(8):
-            onehot[ib * 128 : (ib + 1) * 128, jb * 128 : (jb + 1) * 128] = jnp.where(
+            onehot[pl.ds(row, 128), jb * 128 : (jb + 1) * 128] = jnp.where(
                 wanted == lanes + jb * 128, 1.0, 0.0
             ).astype(BF16)
+        return carry
+
+    lax.fori_loop(0, 8, pick, 0)
 
     coef_copy.wait()
+    for copy in leg_copies[:4]:
+        copy.start()
     packed = coef[...].reshape(2 * ROWS, 128).T
     column = lax.broadcasted_iota(I32, (1, 2 * ROWS), 1)
     row_id, pair_id = column >> 1, column & 1
@@ -98,23 +103,37 @@
 
     pl.semaphore_wait(barrier, 10)
     signal(ring_sems.at[0])
-    for jp in range(4):
-        leg_copies[2 * jp].wait()
-        leg_copies[2 * jp + 1].wait()
+    for copy in leg_copies[4:]:
+        copy.start()
+
+    def legs(jp, carry):
+        for jt in range(2):
+            pltpu.make_async_copy(leg_hbm.at[:, 2 * jp + jt], leg.at[2 * jp + jt], leg_sem.at[2 * jp + jt]).wait()
         table = jnp.concatenate(
             [leg[2 * jp].reshape(2 * ROWS, 128), leg[2 * jp + 1].reshape(2 * ROWS, 128)], axis=1
         )
-        spec[:, jp * 256 : (jp + 1) * 256] = jnp.dot(
+        spec[:, pl.ds(pl.multiple_of(jp * 256, 256), 256)] = jnp.dot(
             stacked[...], table, preferred_element_type=F32
         ).astype(BF16)
-        if jp == 2:
-            pl.semaphore_wait(ring_sems.at[0], 10)
-            signal(ring_sems.at[1])
-    outbox[...] = (
-        lax.dot_general(onehot[...], spec[...], (((1,), (1,)), ((), ())), preferred_element_type=F32)
-        .reshape(NBLK, 8, COLS)
-        .astype(BF16)
-    )
+        return carry
+
+    lax.fori_loop(0, 3, legs, 0)
+    pl.semaphore_wait(ring_sems.at[0], 10)
+    signal(ring_sems.at[1])
+    lax.fori_loop(3, 4, legs, 0)
+
+    def choose(ib, carry):
+        row = pl.multiple_of(ib * 256, 256)
+        outbox[pl.ds(pl.multiple_of(ib * 32, 32), 32)] = (
+            lax.dot_general(
+                onehot[pl.ds(row, 256), :], spec[...], (((1,), (1,)), ((), ())), preferred_element_type=F32
+            )
+            .reshape(32, 8, COLS)
+            .astype(BF16)
+        )
+        return carry
+
+    lax.fori_loop(0, 4, choose, 0)
 
     def send(dz, dy, dx, dc):
         target = at(dz, dy, dx, dc)
@@ -224,23 +243,34 @@
             device_id={"blk": at(d, 0, 0, 0)}, device_id_type=MESH,
         ).start()
 
-    for back in (0, 2, 1, 3):
-        plane = (z + 4 - back) % 4
-        count = PLANE - 1 if back == 0 else PLANE
-        come = pltpu.make_async_remote_copy(
+    def landed(back, count):
+        pltpu.make_async_remote_copy(
             src_ref=outbox.at[pl.ds(0, count)], dst_ref=inbox.at[pl.ds(0, count)],
             send_sem=send_sem, recv_sem=recv_sem.at[back], device_id={"blk": at(0, 0, 0, 1)}, device_id_type=MESH,
-        )
-        come.wait_recv()
+        ).wait_recv()
+
+    def build(step, carry):
+        back = (2 * step) % 3 + step // 3 * 3
+        plane = (z + 4 - back) % 4
+        @pl.when(step == 0)
+        def _():
+            landed(0, PLANE - 1)
+
+        @pl.when(step > 0)
+        def _():
+            landed(back, PLANE)
+
         for g in range(4):
-            wide[g] = (
-                inbox[pl.ds(plane * PLANE, PLANE), :, g * 128 : (g + 1) * 128].astype(F32).reshape(256, 128)
-            )
+            wide[g] = inbox[pl.ds(plane * PLANE, PLANE), :, g * 128 : (g + 1) * 128].astype(F32).reshape(256, 128)
+        col = pl.multiple_of(back * 128, 128)
         for i in range(8):
             block = jnp.concatenate([wide[g, pl.ds(i, PLANE, stride=8), :] for g in range(4)], axis=0)
             block = block.T.astype(BF16)
-            even_x[i * 64 : (i + 1) * 64, back * 128 : (back + 1) * 128] = block[:64]
-            odd_x[i * 64 : (i + 1) * 64, back * 128 : (back + 1) * 128] = block[64:]
+            even_x[i * 64 : (i + 1) * 64, pl.ds(col, 128)] = block[:64]
+            odd_x[i * 64 : (i + 1) * 64, pl.ds(col, 128)] = block[64:]
+        return carry
+
+    lax.fori_loop(0, 4, build, 0)
 
     told = pltpu.make_async_remote_copy(
         src_ref=e_all.at[pl.ds(0, 3)], dst_ref=e_all.at[pl.ds(0, 3)],
@@ -262,22 +292,28 @@
     steps = HALF // 256
 
     def out_copy(step, half):
+        first = pl.multiple_of(half * HALF + step * 256, 256)
         return pltpu.make_async_copy(
-            tile.at[step, half],
-            potential_hbm.at[:, :, pl.ds(half * HALF + step * 256, 256)],
-            tile_sems.at[step, half],
+            tile.at[step, half], potential_hbm.at[:, :, pl.ds(first, 256)], tile_sems.at[step, half]
         )
 
-    for n in range(steps):
-        evens = jnp.dot(even_x[...], basis[:COLS, n * 256 : (n + 1) * 256], preferred_element_type=F32)
-        odds = jnp.dot(odd_x[...], basis[COLS:, n * 256 : (n + 1) * 256], preferred_element_type=F32)
+    def columns(n, carry):
+        at = pl.ds(pl.multiple_of(n * 256, 256), 256)
+        evens = jnp.dot(even_x[...], basis[:COLS, at], preferred_element_type=F32)
+        odds = jnp.dot(odd_x[...], basis[COLS:, at], preferred_element_type=F32)
         tile[n, 0] = (evens + odds).astype(BF16).reshape(8, FIELDS, 256)
         tile[n, 1] = (evens - odds).astype(BF16).reshape(8, FIELDS, 256)
         for half in range(2):
             out_copy(n, half).start()
-    for n in range(steps):
+        return carry
+
+    def finish(n, carry):
         for half in range(2):
             out_copy(n, half).wait()
+        return carry
+
+    lax.fori_loop(0, steps, columns, 0)
+    lax.fori_loop(0, steps, finish, 0)
 
 
 def shards(load_coef, legendre, slab_orders, cycle_rows):

time: 50.8 us -> 47.5 us (0.935)
  Pallas kernels: 49.9 us -> 46.8 us
    pallas_call x1, Pallas kernels: 46.1 us -> 41.7 us  [shards(): pl.pallas_call(exchange, out_shape=(jax.ShapeDtypeStruct((COLS, COLS), BF...]
    pallas_call x1, Pallas kernels: 3.81 us -> 5.14 us  [shards(): pl.pallas_call(synthesize, out_shape=(jax.ShapeDtypeStruct((8, FIELDS, NL...]
where the time goes in v1:
time: 47.5 us; the launch traced here: 47.4 us
  Pallas kernels  46.8 us (99%)
  between operations  0.64 us (1%)
    pallas_call x1, Pallas kernels, shards(): pl.pallas_call(exchange, out_shape=(jax.ShapeDtypeStruct((COLS, COLS), BF...  41.7 us
    pallas_call x1, Pallas kernels, shards(): pl.pallas_call(synthesize, out_shape=(jax.ShapeDtypeStruct((8, FIELDS, NL...  5.14 us

profile of v1, /device:TPU:33, one launch (start us, length us, event | category | flops | bytes accessed | tf_op | source)
XLA Modules:
  0.0 47.4 jit_solution(6247587438542420131)
XLA Ops:
  0.6 41.7 %exchange.1 = (bf16[512,512]{1,0:T(8,128)(2,1)S(1)}, bf16[512,512]{1,0:T(8,128)(2,1)S(1)}, bf16[1024,2048]{1,0:T(8,128)(2,1)S(1)}, f32[1,128]{1,0:T(1,128)S(1)}) custom-call(s32[2,128]{1,0:T(2,128)} %bitcast.12, s32[8,128]{1,0:T(8,128)} %bitcast.11, bf16[2049,2,128]{2,1,0:T(2,128)(2,1)} %bitcast.10, bf16[2049,8,2,128]{3,2,1,0:T(2,128)(2,1)} %bitcast.9), custom_call_target="tpu_custom_call" | custom-call | tf_op jit(solution)/shard_map/exchange/pallas_call | solution.py:324
  42.3 5.1 %synthesize.1 = (bf16[8,64,4096]{2,1,0:T(8,128)(2,1)}, f32[1,64]{1,0:T(1,128)}) custom-call(f32[1,128]{1,0:T(1,128)S(1)} %get-tuple-element.8.energy_in, bf16[512,512]{1,0:T(8,128)(2,1)S(1)} %get-tuple-element.9.even_x, bf16[512,512]{1,0:T(8,128)(2,1)S(1)} %get-tuple-element.10.odd_x, bf16[1024,2048]{1,0:T(8,128)(2,1)S(1)} %get-tuple-element.11.basis), custom_call_target="tpu_custom_call" | custom-call | tf_op jit(solution)/shard_map/synthesize/pallas_call | solution.py:362

commit v2 on v1

--- a/solution.py
+++ b/solution.py
@@ -39,8 +39,8 @@
 
 def exchange(
     orders_hbm, cycles_hbm, coef_hbm, leg_hbm,
-    even_x, odd_x, basis, energy_ref,
-    orders_v, cycles, coef, leg, stacked, spec, onehot, outbox, inbox, wide, order_cols, e_mine, e_plane, e_all,
+    even_x, odd_x, basis, evens, odds, energy_ref,
+    orders_v, cycles, coef, leg, first_x, stacked, spec, onehot, outbox, inbox, wide, order_cols, e_mine, e_plane, e_all,
     small_sems, coef_sem, leg_sem, send_sem, recv_sem, e_sems, ring_sems,
 ):
     me = lax.axis_index("blk")
@@ -205,10 +205,13 @@
 
     lax.fori_loop(1, PLANE, tell, 0)
 
+    def back_of(slot):
+        return (2 * slot) % 3 + slot // 3 * 3
+
     def basis_step(step, carry):
         a, part = step // 16, step % 16
-        back, sub = part // 4, part % 4
-        first = (z + 4 - back) % 4 * 64 + sub * 16
+        slot, sub = part // 4, part % 4
+        first = (z + 4 - back_of(slot)) % 4 * 64 + sub * 16
         col = pl.multiple_of(a * 128, 128)
         for p in range(2):
             order = order_cols[pl.ds(first + p, 8, stride=2), :]
@@ -218,9 +221,9 @@
                 m = even if parity == 0 else DEGREE - even
                 cosine, sine = sincos(m * k)
                 factor = jnp.where(m == 0, 1.0, 2.0)
-                row = pl.multiple_of(parity * COLS + back * 128 + p * 64 + sub * 8, 8)
+                row = pl.multiple_of(parity * COLS + slot * 128 + p * 64 + sub * 8, 8)
                 basis[pl.ds(row, 8), pl.ds(col, 128)] = (factor * cosine).astype(BF16)
-                row = pl.multiple_of(parity * COLS + back * 128 + p * 64 + 32 + sub * 8, 8)
+                row = pl.multiple_of(parity * COLS + slot * 128 + p * 64 + 32 + sub * 8, 8)
                 basis[pl.ds(row, 8), pl.ds(col, 128)] = (-factor * sine).astype(BF16)
         return carry
 
@@ -249,28 +252,43 @@
             send_sem=send_sem, recv_sem=recv_sem.at[back], device_id={"blk": at(0, 0, 0, 1)}, device_id_type=MESH,
         ).wait_recv()
 
-    def build(step, carry):
-        back = (2 * step) % 3 + step // 3 * 3
+    def build(slot, even_to, odd_to):
+        back = back_of(slot)
         plane = (z + 4 - back) % 4
-        @pl.when(step == 0)
+        @pl.when(slot == 0)
         def _():
             landed(0, PLANE - 1)
 
-        @pl.when(step > 0)
+        @pl.when(slot > 0)
         def _():
             landed(back, PLANE)
 
         for g in range(4):
             wide[g] = inbox[pl.ds(plane * PLANE, PLANE), :, g * 128 : (g + 1) * 128].astype(F32).reshape(256, 128)
-        col = pl.multiple_of(back * 128, 128)
+        col = pl.multiple_of(slot % 2 * 128, 128)
         for i in range(8):
             block = jnp.concatenate([wide[g, pl.ds(i, PLANE, stride=8), :] for g in range(4)], axis=0)
             block = block.T.astype(BF16)
-            even_x[i * 64 : (i + 1) * 64, pl.ds(col, 128)] = block[:64]
-            odd_x[i * 64 : (i + 1) * 64, pl.ds(col, 128)] = block[64:]
-        return carry
-
-    lax.fori_loop(0, 4, build, 0)
+            even_to[i * 64 : (i + 1) * 64, pl.ds(col, 128)] = block[:64]
+            odd_to[i * 64 : (i + 1) * 64, pl.ds(col, 128)] = block[64:]
+
+    def build_first(slot, carry):
+        build(slot, first_x.at[0], first_x.at[1])
+        return carry
+
+    def build_last(slot, carry):
+        build(slot, even_x, odd_x)
+        return carry
+
+    def sum_first(n, carry):
+        cols = pl.ds(pl.multiple_of(n * 256, 256), 256)
+        evens[:, cols] = jnp.dot(first_x[0], basis[:256, cols], preferred_element_type=F32)
+        odds[:, cols] = jnp.dot(first_x[1], basis[COLS : COLS + 256, cols], preferred_element_type=F32)
+        return carry
+
+    lax.fori_loop(0, 2, build_first, 0)
+    lax.fori_loop(0, 8, sum_first, 0)
+    lax.fori_loop(2, 4, build_last, 0)
 
     told = pltpu.make_async_remote_copy(
         src_ref=e_all.at[pl.ds(0, 3)], dst_ref=e_all.at[pl.ds(0, 3)],
@@ -286,34 +304,24 @@
     sent.wait_send()
 
 
-def synthesize(energy_in, even_x, odd_x, basis, potential_hbm, energy_ref, tile, tile_sems):
+def synthesize(energy_in, even_x, odd_x, basis, evens, odds, potential_hbm, energy_ref, tile, tile_sems):
     both = energy_in[...]
     energy_ref[...] = (both[:, :FIELDS] + both[:, FIELDS:]) * (1.0 / NLAT)
     steps = HALF // 256
-
-    def out_copy(step, half):
-        first = pl.multiple_of(half * HALF + step * 256, 256)
-        return pltpu.make_async_copy(
-            tile.at[step, half], potential_hbm.at[:, :, pl.ds(first, 256)], tile_sems.at[step, half]
-        )
-
-    def columns(n, carry):
-        at = pl.ds(pl.multiple_of(n * 256, 256), 256)
-        evens = jnp.dot(even_x[...], basis[:COLS, at], preferred_element_type=F32)
-        odds = jnp.dot(odd_x[...], basis[COLS:, at], preferred_element_type=F32)
-        tile[n, 0] = (evens + odds).astype(BF16).reshape(8, FIELDS, 256)
-        tile[n, 1] = (evens - odds).astype(BF16).reshape(8, FIELDS, 256)
+    copies = []
+    for n in range(steps):
+        cols = slice(n * 256, (n + 1) * 256)
+        even = evens[:, cols] + jnp.dot(even_x[...], basis[256:COLS, cols], preferred_element_type=F32)
+        odd = odds[:, cols] + jnp.dot(odd_x[...], basis[COLS + 256 :, cols], preferred_element_type=F32)
         for half in range(2):
-            out_copy(n, half).start()
-        return carry
-
-    def finish(n, carry):
-        for half in range(2):
-            out_copy(n, half).wait()
-        return carry
-
-    lax.fori_loop(0, steps, columns, 0)
-    lax.fori_loop(0, steps, finish, 0)
+            tile[n, half] = (even + odd if half == 0 else even - odd).astype(BF16).reshape(8, FIELDS, 256)
+            copy = pltpu.make_async_copy(
+                tile.at[n, half], potential_hbm.at[:, :, pl.ds(half * HALF + n * 256, 256)], tile_sems.at[n, half]
+            )
+            copy.start()
+            copies.append(copy)
+    for copy in copies:
+        copy.wait()
 
 
 def shards(load_coef, legendre, slab_orders, cycle_rows):
@@ -321,21 +329,24 @@
     vmem = pl.BlockSpec(memory_space=pltpu.VMEM)
     coef = load_coef.transpose(1, 0, 2)
     table = legendre.transpose(1, 0, 2).reshape(ROWS, 2, 8, 128).transpose(0, 2, 1, 3)
-    even_x, odd_x, basis, energy = pl.pallas_call(
+    even_x, odd_x, basis, evens, odds, energy = pl.pallas_call(
         exchange,
         out_shape=(
-            jax.ShapeDtypeStruct((COLS, COLS), BF16),
-            jax.ShapeDtypeStruct((COLS, COLS), BF16),
+            jax.ShapeDtypeStruct((COLS, 256), BF16),
+            jax.ShapeDtypeStruct((COLS, 256), BF16),
             jax.ShapeDtypeStruct((2 * COLS, HALF), BF16),
+            jax.ShapeDtypeStruct((COLS, HALF), F32),
+            jax.ShapeDtypeStruct((COLS, HALF), F32),
             jax.ShapeDtypeStruct((1, 128), F32),
         ),
         in_specs=[pl.BlockSpec(memory_space=pltpu.HBM)] * 4,
-        out_specs=(vmem, vmem, vmem, vmem),
+        out_specs=(vmem,) * 6,
         scratch_shapes=[
             pltpu.VMEM((2, 128), I32),
             pltpu.VMEM((8, 128), I32),
             pltpu.VMEM((ROWS, 2, 128), BF16),
             pltpu.VMEM((8, ROWS, 2, 128), BF16),
+            pltpu.VMEM((2, COLS, 256), BF16),
             pltpu.VMEM((COLS, 2 * ROWS), BF16),
             pltpu.VMEM((COLS, NLAT), BF16),
             pltpu.VMEM((NLAT, NLAT), BF16),
@@ -355,7 +366,7 @@
             pltpu.SemaphoreType.REGULAR((3,)),
         ],
         compiler_params=pltpu.CompilerParams(
-            collective_id=0, has_side_effects=True, vmem_limit_bytes=44 * 1024 * 1024
+            collective_id=0, has_side_effects=True, vmem_limit_bytes=36 * 1024 * 1024
         ),
         name="exchange",
     )(*[pltpu.with_memory_space_constraint(a, pltpu.HBM) for a in (slab_orders.reshape(2, 128), cycle_rows.reshape(8, 128), coef, table)])
@@ -365,15 +376,15 @@
             jax.ShapeDtypeStruct((8, FIELDS, NLON), BF16),
             jax.ShapeDtypeStruct((1, FIELDS), F32),
         ),
-        in_specs=[vmem, vmem, vmem, vmem],
+        in_specs=[vmem] * 6,
         out_specs=(any_space, vmem),
         scratch_shapes=[
             pltpu.VMEM((8, 2, 8, FIELDS, 256), BF16),
             pltpu.SemaphoreType.DMA((8, 2)),
         ],
-        compiler_params=pltpu.CompilerParams(vmem_limit_bytes=24 * 1024 * 1024),
+        compiler_params=pltpu.CompilerParams(vmem_limit_bytes=20 * 1024 * 1024),
         name="synthesize",
-    )(energy, even_x, odd_x, basis)
+    )(energy, even_x, odd_x, basis, evens, odds)
     return potential, energy.reshape(FIELDS)
 
 

time: 47.5 us -> 46.6 us (0.981)
  the two profiles are of different devices: /device:TPU:33 before, /device:TPU:1 now
where the time goes in v2:
time: 46.6 us; the launch traced here: 46.5 us
  Pallas kernels  45.8 us (98%)
  between operations  0.64 us (1%)
    pallas_call x1, Pallas kernels, shards(): pl.pallas_call(exchange, out_shape=(jax.ShapeDtypeStruct((COLS, 256), BF1...  42.9 us
    pallas_call x1, Pallas kernels, shards(): pl.pallas_call(synthesize, out_shape=(jax.ShapeDtypeStruct((8, FIELDS, NL...  2.95 us

profile of v2, /device:TPU:1, one launch (start us, length us, event | category | flops | bytes accessed | tf_op | source)
XLA Modules:
  0.0 46.5 jit_solution(12304099119244878923)
XLA Ops:
  0.6 42.9 %exchange.1 = (bf16[512,256]{1,0:T(8,128)(2,1)S(1)}, bf16[512,256]{1,0:T(8,128)(2,1)S(1)}, bf16[1024,2048]{1,0:T(8,128)(2,1)S(1)}, f32[512,2048]{1,0:T(8,128)S(1...) custom-call(s32[2,128]{1,0:T(2,128)} %bitcast.12, s32[8,128]{1,0:T(8,128)} %bitcast.11, bf16[2049,2,128]{2,1,0:T(2,128)(2,1)} %bitcast.10, ...), custom_call_target="tpu_custom_call" | custom-call | tf_op jit(solution)/shard_map/exchange/pallas_call | solution.py:332
  43.5 3.0 %synthesize.1 = (bf16[8,64,4096]{2,1,0:T(8,128)(2,1)}, f32[1,64]{1,0:T(1,128)}) custom-call(f32[1,128]{1,0:T(1,128)S(1)} %get-tuple-element.10.energy_in, bf16[512,256]{1,0:T(8,128)(2,1)S(1)} %get-tuple-element.11.even_x, bf16[512,256]{1,0:T(8,128)(2,1)S(1)} %get-tuple-element.12.odd_x, bf16[1024,2048]{1,0:T(8,128)(2,1)S(1)} %get-tuple-element.13.basis, ...), custom_call_target="tpu_custom_call" | custom-call | tf_op jit(solution)/shard_map/synthesize/pallas_call | solution.py:373

commit v3 on v2

--- a/solution.py
+++ b/solution.py
@@ -195,6 +195,34 @@
     e_mine[0] = energy
     e_plane[place] = energy
 
+    def back_of(slot):
+        late = slot // 2
+        swap = (slot % 2 + z + 1) % 2
+        return (1 - late) * 2 * slot + late * (1 + 2 * swap)
+
+    lane = lax.broadcasted_iota(I32, (16, 128), 1)
+
+    def basis_step(step, carry):
+        slot, sub = step // 2, step % 2
+        first = (z + 4 - back_of(slot)) % 4 * 64 + sub * 32
+        for p in range(2):
+            order = order_cols[pl.ds(first + p, 16, stride=2), :]
+            even = jnp.where((order & 1) == 1, DEGREE - order, order)
+            for parity in range(2):
+                m = even if parity == 0 else DEGREE - even
+                cosine, sine = sincos(m * lane)
+                turn_cos, turn_sin = sincos(m * 128)
+                factor = jnp.where(m == 0, 1.0, 2.0)
+                re, im = factor * cosine, -factor * sine
+                row = pl.multiple_of(parity * COLS + slot * 128 + p * 64 + sub * 16, 16)
+                for a in range(HALF // 128):
+                    basis[pl.ds(row, 16), a * 128 : (a + 1) * 128] = re.astype(BF16)
+                    basis[pl.ds(row + 32, 16), a * 128 : (a + 1) * 128] = im.astype(BF16)
+                    re, im = re * turn_cos + im * turn_sin, im * turn_cos - re * turn_sin
+        return carry
+
+    lax.fori_loop(0, 8, basis_step, 0)
+
     def tell(t, carry):
         target = at(0, t // 8, (t // 2) % 4, t % 2)
         pltpu.make_async_remote_copy(
@@ -205,30 +233,47 @@
 
     lax.fori_loop(1, PLANE, tell, 0)
 
-    def back_of(slot):
-        return (2 * slot) % 3 + slot // 3 * 3
-
-    def basis_step(step, carry):
-        a, part = step // 16, step % 16
-        slot, sub = part // 4, part % 4
-        first = (z + 4 - back_of(slot)) % 4 * 64 + sub * 16
-        col = pl.multiple_of(a * 128, 128)
-        for p in range(2):
-            order = order_cols[pl.ds(first + p, 8, stride=2), :]
-            even = jnp.where((order & 1) == 1, DEGREE - order, order)
-            k = lax.broadcasted_iota(I32, (8, 128), 1) + a * 128
-            for parity in range(2):
-                m = even if parity == 0 else DEGREE - even
-                cosine, sine = sincos(m * k)
-                factor = jnp.where(m == 0, 1.0, 2.0)
-                row = pl.multiple_of(parity * COLS + slot * 128 + p * 64 + sub * 8, 8)
-                basis[pl.ds(row, 8), pl.ds(col, 128)] = (factor * cosine).astype(BF16)
-                row = pl.multiple_of(parity * COLS + slot * 128 + p * 64 + 32 + sub * 8, 8)
-                basis[pl.ds(row, 8), pl.ds(col, 128)] = (-factor * sine).astype(BF16)
-        return carry
-
-    lax.fori_loop(0, 256, basis_step, 0)
-
+    def landed(back, count):
+        pltpu.make_async_remote_copy(
+            src_ref=outbox.at[pl.ds(0, count)], dst_ref=inbox.at[pl.ds(0, count)],
+            send_sem=send_sem, recv_sem=recv_sem.at[back], device_id={"blk": at(0, 0, 0, 1)}, device_id_type=MESH,
+        ).wait_recv()
+
+    def build(slot, even_to, odd_to):
+        back = back_of(slot)
+        plane = (z + 4 - back) % 4
+        @pl.when(slot == 0)
+        def _():
+            landed(0, PLANE - 1)
+
+        @pl.when(slot > 0)
+        def _():
+            landed(back, PLANE)
+
+        for g in range(4):
+            wide[g] = inbox[pl.ds(plane * PLANE, PLANE), :, g * 128 : (g + 1) * 128].astype(F32).reshape(256, 128)
+        col = pl.multiple_of(slot % 2 * 128, 128)
+        for i in range(8):
+            block = jnp.concatenate([wide[g, pl.ds(i, PLANE, stride=8), :] for g in range(4)], axis=0)
+            block = block.T.astype(BF16)
+            even_to[i * 64 : (i + 1) * 64, pl.ds(col, 128)] = block[:64]
+            odd_to[i * 64 : (i + 1) * 64, pl.ds(col, 128)] = block[64:]
+
+    def build_first(slot, carry):
+        build(slot, first_x.at[0], first_x.at[1])
+        return carry
+
+    def build_last(slot, carry):
+        build(slot, even_x, odd_x)
+        return carry
+
+    def sum_first(n, carry):
+        cols = pl.ds(pl.multiple_of(n * 256, 256), 256)
+        evens[:, cols] = jnp.dot(first_x[0], basis[:256, cols], preferred_element_type=F32)
+        odds[:, cols] = jnp.dot(first_x[1], basis[COLS : COLS + 256, cols], preferred_element_type=F32)
+        return carry
+
+    lax.fori_loop(0, 2, build_first, 0)
     told = pltpu.make_async_remote_copy(
         src_ref=e_plane.at[pl.ds(0, PLANE - 1)], dst_ref=e_plane.at[pl.ds(0, PLANE - 1)],
         send_sem=e_sems.at[0], recv_sem=e_sems.at[1], device_id={"blk": at(0, 0, 0, 1)}, device_id_type=MESH,
@@ -240,54 +285,14 @@
         total = total + e_plane[s]
     e_mine[1] = total
     e_all[z] = total
+    lax.fori_loop(0, 8, sum_first, 0)
+
     for d in range(1, 4):
         pltpu.make_async_remote_copy(
             src_ref=e_mine.at[1], dst_ref=e_all.at[z], send_sem=e_sems.at[2], recv_sem=e_sems.at[3],
             device_id={"blk": at(d, 0, 0, 0)}, device_id_type=MESH,
         ).start()
 
-    def landed(back, count):
-        pltpu.make_async_remote_copy(
-            src_ref=outbox.at[pl.ds(0, count)], dst_ref=inbox.at[pl.ds(0, count)],
-            send_sem=send_sem, recv_sem=recv_sem.at[back], device_id={"blk": at(0, 0, 0, 1)}, device_id_type=MESH,
-        ).wait_recv()
-
-    def build(slot, even_to, odd_to):
-        back = back_of(slot)
-        plane = (z + 4 - back) % 4
-        @pl.when(slot == 0)
-        def _():
-            landed(0, PLANE - 1)
-
-        @pl.when(slot > 0)
-        def _():
-            landed(back, PLANE)
-
-        for g in range(4):
-            wide[g] = inbox[pl.ds(plane * PLANE, PLANE), :, g * 128 : (g + 1) * 128].astype(F32).reshape(256, 128)
-        col = pl.multiple_of(slot % 2 * 128, 128)
-        for i in range(8):
-            block = jnp.concatenate([wide[g, pl.ds(i, PLANE, stride=8), :] for g in range(4)], axis=0)
-            block = block.T.astype(BF16)
-            even_to[i * 64 : (i + 1) * 64, pl.ds(col, 128)] = block[:64]
-            odd_to[i * 64 : (i + 1) * 64, pl.ds(col, 128)] = block[64:]
-
-    def build_first(slot, carry):
-        build(slot, first_x.at[0], first_x.at[1])
-        return carry
-
-    def build_last(slot, carry):
-        build(slot, even_x, odd_x)
-        return carry
-
-    def sum_first(n, carry):
-        cols = pl.ds(pl.multiple_of(n * 256, 256), 256)
-        evens[:, cols] = jnp.dot(first_x[0], basis[:256, cols], preferred_element_type=F32)
-        odds[:, cols] = jnp.dot(first_x[1], basis[COLS : COLS + 256, cols], preferred_element_type=F32)
-        return carry
-
-    lax.fori_loop(0, 2, build_first, 0)
-    lax.fori_loop(0, 8, sum_first, 0)
     lax.fori_loop(2, 4, build_last, 0)
 
     told = pltpu.make_async_remote_copy(

time: 46.6 us -> 47.8 us (1.026)
  Pallas kernels: 45.8 us -> 47.1 us
    pallas_call x1, Pallas kernels: 42.9 us -> 44.1 us  [shards(): pl.pallas_call(exchange, out_shape=(jax.ShapeDtypeStruct((COLS, 256), BF1...]
where the time goes in v3:
time: 47.8 us; the launch traced here: 47.7 us
  Pallas kernels  47.1 us (99%)
  between operations  0.64 us (1%)
    pallas_call x1, Pallas kernels, shards(): pl.pallas_call(exchange, out_shape=(jax.ShapeDtypeStruct((COLS, 256), BF1...  44.1 us
    pallas_call x1, Pallas kernels, shards(): pl.pallas_call(synthesize, out_shape=(jax.ShapeDtypeStruct((8, FIELDS, NL...  2.96 us

profile of v3, /device:TPU:1, one launch (start us, length us, event | category | flops | bytes accessed | tf_op | source)
XLA Modules:
  0.0 47.7 jit_solution(6219858128583940283)
XLA Ops:
  0.6 44.1 %exchange.1 = (bf16[512,256]{1,0:T(8,128)(2,1)S(1)}, bf16[512,256]{1,0:T(8,128)(2,1)S(1)}, bf16[1024,2048]{1,0:T(8,128)(2,1)S(1)}, f32[512,2048]{1,0:T(8,128)S(1...) custom-call(s32[2,128]{1,0:T(2,128)} %bitcast.12, s32[8,128]{1,0:T(8,128)} %bitcast.11, bf16[2049,2,128]{2,1,0:T(2,128)(2,1)} %bitcast.10, ...), custom_call_target="tpu_custom_call" | custom-call | tf_op jit(solution)/shard_map/exchange/pallas_call | solution.py:337
  44.7 3.0 %synthesize.1 = (bf16[8,64,4096]{2,1,0:T(8,128)(2,1)}, f32[1,64]{1,0:T(1,128)}) custom-call(f32[1,128]{1,0:T(1,128)S(1)} %get-tuple-element.10.energy_in, bf16[512,256]{1,0:T(8,128)(2,1)S(1)} %get-tuple-element.11.even_x, bf16[512,256]{1,0:T(8,128)(2,1)S(1)} %get-tuple-element.12.odd_x, bf16[1024,2048]{1,0:T(8,128)(2,1)S(1)} %get-tuple-element.13.basis, ...), custom_call_target="tpu_custom_call" | custom-call | tf_op jit(solution)/shard_map/synthesize/pallas_call | solution.py:378

commit v4 on v3

--- a/solution.py
+++ b/solution.py
@@ -160,23 +160,15 @@
         else:
             lax.fori_loop(0, count, one, 0)
 
-    across = (2, 1, 3)
-    send_all(across, (), 0)
-    send_all((2, 1, 3, 0), (2,), 0)
-    send_all((2, 1, 3, 0), (1,), 0)
-    send_all((2, 1, 3, 0), (), 1)
-    for axes, flip in (((1, 2), 0), ((1,), 1), ((2,), 1)):
-        send_all((0,), axes, flip)
-    pl.semaphore_wait(ring_sems.at[1], 10)
-    signal(ring_sems.at[2])
-    for axes, flip in (((1, 2), 0), ((1,), 1), ((2,), 1)):
-        send_all((2,), axes, flip)
-    send_all((0,), (1, 2), 1)
-    pl.semaphore_wait(ring_sems.at[2], 10)
-    send_all((2,), (1, 2), 1)
-    for axes, flip in (((1, 2), 0), ((1,), 1), ((2,), 1), ((1, 2), 1)):
-        send_all((1, 3), axes, flip)
-    inbox[me] = outbox[me]
+    beside = 1 + 2 * (z % 2)
+    across = 4 - beside
+    send_all((beside, 0, across), (2,), 0)
+    send_all((beside, 0, across), (1,), 0)
+    send_all((beside, 0, across), (), 1)
+    send_all((beside, across), (), 0)
+    send_all((0,), (1, 2), 0)
+    send_all((0,), (1,), 1)
+    send_all((0,), (2,), 1)
 
     place = me % PLANE
     is_even = lax.broadcasted_iota(I32, (1, 128), 1) < FIELDS
@@ -193,12 +185,27 @@
             weight = jnp.where(is_even, jnp.where(has_zero, 1.0 - part, 2.0), 2.0)
             energy = energy + weight * jnp.sum(squares.T, axis=0, keepdims=True)
     e_mine[0] = energy
-    e_plane[place] = energy
+    e_all[z] = energy
+    pl.semaphore_wait(ring_sems.at[1], 10)
+    signal(ring_sems.at[2])
+    for axes, flip in (((1, 2), 0), ((1,), 1), ((2,), 1)):
+        send_all((beside, across), axes, flip)
+    send_all((0,), (1, 2), 1)
+
+    for d in range(1, 4):
+        pltpu.make_async_remote_copy(
+            src_ref=e_mine.at[0], dst_ref=e_all.at[z], send_sem=e_sems.at[2], recv_sem=e_sems.at[3],
+            device_id={"blk": at(d, 0, 0, 0)}, device_id_type=MESH,
+        ).start()
+    pl.semaphore_wait(ring_sems.at[2], 10)
+    send_all((beside, across), (1, 2), 1)
+    for axes, flip in (((), 0), ((2,), 0), ((1,), 0), ((), 1), ((1, 2), 0), ((1,), 1), ((2,), 1), ((1, 2), 1)):
+        send_all((2,), axes, flip)
+    inbox[me] = outbox[me]
+
 
     def back_of(slot):
-        late = slot // 2
-        swap = (slot % 2 + z + 1) % 2
-        return (1 - late) * 2 * slot + late * (1 + 2 * swap)
+        return slot % 2 * across * (1 - slot // 2) + slot // 2 * (beside + slot % 2 * (2 - beside))
 
     lane = lax.broadcasted_iota(I32, (16, 128), 1)
 
@@ -223,36 +230,16 @@
 
     lax.fori_loop(0, 8, basis_step, 0)
 
-    def tell(t, carry):
-        target = at(0, t // 8, (t // 2) % 4, t % 2)
-        pltpu.make_async_remote_copy(
-            src_ref=e_mine.at[0], dst_ref=e_plane.at[place], send_sem=e_sems.at[0], recv_sem=e_sems.at[1],
-            device_id={"blk": target}, device_id_type=MESH,
-        ).start()
-        return carry
-
-    lax.fori_loop(1, PLANE, tell, 0)
-
     def landed(back, count):
         pltpu.make_async_remote_copy(
             src_ref=outbox.at[pl.ds(0, count)], dst_ref=inbox.at[pl.ds(0, count)],
             send_sem=send_sem, recv_sem=recv_sem.at[back], device_id={"blk": at(0, 0, 0, 1)}, device_id_type=MESH,
         ).wait_recv()
 
-    def build(slot, even_to, odd_to):
-        back = back_of(slot)
-        plane = (z + 4 - back) % 4
-        @pl.when(slot == 0)
-        def _():
-            landed(0, PLANE - 1)
-
-        @pl.when(slot > 0)
-        def _():
-            landed(back, PLANE)
-
+    def build(slot, even_to, odd_to, col):
+        plane = (z + 4 - back_of(slot)) % 4
         for g in range(4):
             wide[g] = inbox[pl.ds(plane * PLANE, PLANE), :, g * 128 : (g + 1) * 128].astype(F32).reshape(256, 128)
-        col = pl.multiple_of(slot % 2 * 128, 128)
         for i in range(8):
             block = jnp.concatenate([wide[g, pl.ds(i, PLANE, stride=8), :] for g in range(4)], axis=0)
             block = block.T.astype(BF16)
@@ -260,20 +247,45 @@
             odd_to[i * 64 : (i + 1) * 64, pl.ds(col, 128)] = block[64:]
 
     def build_first(slot, carry):
-        build(slot, first_x.at[0], first_x.at[1])
-        return carry
-
-    def build_last(slot, carry):
-        build(slot, even_x, odd_x)
+        @pl.when(slot == 0)
+        def _():
+            landed(0, PLANE - 1)
+
+        @pl.when(slot > 0)
+        def _():
+            landed(back_of(slot), PLANE)
+
+        build(slot, first_x.at[0], first_x.at[1], pl.multiple_of(slot * 128, 128))
         return carry
 
     def sum_first(n, carry):
         cols = pl.ds(pl.multiple_of(n * 256, 256), 256)
-        evens[:, cols] = jnp.dot(first_x[0], basis[:256, cols], preferred_element_type=F32)
-        odds[:, cols] = jnp.dot(first_x[1], basis[COLS : COLS + 256, cols], preferred_element_type=F32)
-        return carry
-
-    lax.fori_loop(0, 2, build_first, 0)
+        evens[:, cols] = jnp.dot(first_x[0], basis[:384, cols], preferred_element_type=F32)
+        odds[:, cols] = jnp.dot(first_x[1], basis[COLS : COLS + 384, cols], preferred_element_type=F32)
+        return carry
+
+    told = pltpu.make_async_remote_copy(
+        src_ref=e_all.at[pl.ds(0, 3)], dst_ref=e_all.at[pl.ds(0, 3)],
+        send_sem=e_sems.at[2], recv_sem=e_sems.at[3], device_id={"blk": at(0, 0, 0, 1)}, device_id_type=MESH,
+    )
+    told.wait_send()
+    told.wait_recv()
+    column_sum = (e_all[0] + e_all[1]) + (e_all[2] + e_all[3])
+    e_mine[1] = column_sum
+    e_plane[place] = column_sum
+    lax.fori_loop(0, 1, build_first, 0)
+
+    def tell(t, carry):
+        target = at(0, t // 8, (t // 2) % 4, t % 2)
+        pltpu.make_async_remote_copy(
+            src_ref=e_mine.at[1], dst_ref=e_plane.at[place], send_sem=e_sems.at[0], recv_sem=e_sems.at[1],
+            device_id={"blk": target}, device_id_type=MESH,
+        ).start()
+        return carry
+
+    lax.fori_loop(1, PLANE, tell, 0)
+    lax.fori_loop(1, 3, build_first, 0)
+    lax.fori_loop(0, 8, sum_first, 0)
     told = pltpu.make_async_remote_copy(
         src_ref=e_plane.at[pl.ds(0, PLANE - 1)], dst_ref=e_plane.at[pl.ds(0, PLANE - 1)],
         send_sem=e_sems.at[0], recv_sem=e_sems.at[1], device_id={"blk": at(0, 0, 0, 1)}, device_id_type=MESH,
@@ -283,25 +295,10 @@
     total = e_plane[0]
     for s in range(1, PLANE):
         total = total + e_plane[s]
-    e_mine[1] = total
-    e_all[z] = total
-    lax.fori_loop(0, 8, sum_first, 0)
-
-    for d in range(1, 4):
-        pltpu.make_async_remote_copy(
-            src_ref=e_mine.at[1], dst_ref=e_all.at[z], send_sem=e_sems.at[2], recv_sem=e_sems.at[3],
-            device_id={"blk": at(d, 0, 0, 0)}, device_id_type=MESH,
-        ).start()
-
-    lax.fori_loop(2, 4, build_last, 0)
-
-    told = pltpu.make_async_remote_copy(
-        src_ref=e_all.at[pl.ds(0, 3)], dst_ref=e_all.at[pl.ds(0, 3)],
-        send_sem=e_sems.at[2], recv_sem=e_sems.at[3], device_id={"blk": at(0, 0, 0, 1)}, device_id_type=MESH,
-    )
-    told.wait_send()
-    told.wait_recv()
-    energy_ref[...] = (e_all[0] + e_all[1]) + (e_all[2] + e_all[3])
+    energy_ref[...] = total
+
+    landed(2, PLANE)
+    build(3, even_x, odd_x, 0)
     sent = pltpu.make_async_remote_copy(
         src_ref=outbox.at[pl.ds(0, NBLK - 1)], dst_ref=inbox.at[pl.ds(0, NBLK - 1)],
         send_sem=send_sem, recv_sem=recv_sem.at[0], device_id={"blk": at(0, 0, 0, 1)}, device_id_type=MESH,
@@ -316,8 +313,8 @@
     copies = []
     for n in range(steps):
         cols = slice(n * 256, (n + 1) * 256)
-        even = evens[:, cols] + jnp.dot(even_x[...], basis[256:COLS, cols], preferred_element_type=F32)
-        odd = odds[:, cols] + jnp.dot(odd_x[...], basis[COLS + 256 :, cols], preferred_element_type=F32)
+        even = evens[:, cols] + jnp.dot(even_x[...], basis[384:COLS, cols], preferred_element_type=F32)
+        odd = odds[:, cols] + jnp.dot(odd_x[...], basis[COLS + 384 :, cols], preferred_element_type=F32)
         for half in range(2):
             tile[n, half] = (even + odd if half == 0 else even - odd).astype(BF16).reshape(8, FIELDS, 256)
             copy = pltpu.make_async_copy(
@@ -337,8 +334,8 @@
     even_x, odd_x, basis, evens, odds, energy = pl.pallas_call(
         exchange,
         out_shape=(
-            jax.ShapeDtypeStruct((COLS, 256), BF16),
-            jax.ShapeDtypeStruct((COLS, 256), BF16),
+            jax.ShapeDtypeStruct((COLS, 128), BF16),
+            jax.ShapeDtypeStruct((COLS, 128), BF16),
             jax.ShapeDtypeStruct((2 * COLS, HALF), BF16),
             jax.ShapeDtypeStruct((COLS, HALF), F32),
             jax.ShapeDtypeStruct((COLS, HALF), F32),
@@ -351,7 +348,7 @@
             pltpu.VMEM((8, 128), I32),
             pltpu.VMEM((ROWS, 2, 128), BF16),
             pltpu.VMEM((8, ROWS, 2, 128), BF16),
-            pltpu.VMEM((2, COLS, 256), BF16),
+            pltpu.VMEM((2, COLS, 384), BF16),
             pltpu.VMEM((COLS, 2 * ROWS), BF16),
             pltpu.VMEM((COLS, NLAT), BF16),
             pltpu.VMEM((NLAT, NLAT), BF16),

time: 47.8 us -> 47.7 us (level)
  no operation moved by 1% of the time
where the time goes in v4:
time: 47.7 us; the launch traced here: 47.6 us
  Pallas kernels  46.9 us (98%)
  between operations  0.64 us (1%)
    pallas_call x1, Pallas kernels, shards(): pl.pallas_call(exchange, out_shape=(jax.ShapeDtypeStruct((COLS, 128), BF1...  44 us
    pallas_call x1, Pallas kernels, shards(): pl.pallas_call(synthesize, out_shape=(jax.ShapeDtypeStruct((8, FIELDS, NL...  2.93 us

profile of v4, /device:TPU:1, one launch (start us, length us, event | category | flops | bytes accessed | tf_op | source)
XLA Modules:
  0.0 47.6 jit_solution(9269105243813967041)
XLA Ops:
  0.6 44.0 %exchange.1 = (bf16[512,128]{1,0:T(8,128)(2,1)S(1)}, bf16[512,128]{1,0:T(8,128)(2,1)S(1)}, bf16[1024,2048]{1,0:T(8,128)(2,1)S(1)}, f32[512,2048]{1,0:T(8,128)S(1...) custom-call(s32[2,128]{1,0:T(2,128)} %bitcast.12, s32[8,128]{1,0:T(8,128)} %bitcast.11, bf16[2049,2,128]{2,1,0:T(2,128)(2,1)} %bitcast.10, ...), custom_call_target="tpu_custom_call" | custom-call | tf_op jit(solution)/shard_map/exchange/pallas_call | solution.py:334
  44.6 2.9 %synthesize.1 = (bf16[8,64,4096]{2,1,0:T(8,128)(2,1)}, f32[1,64]{1,0:T(1,128)}) custom-call(f32[1,128]{1,0:T(1,128)S(1)} %get-tuple-element.10.energy_in, bf16[512,128]{1,0:T(8,128)(2,1)S(1)} %get-tuple-element.11.even_x, bf16[512,128]{1,0:T(8,128)(2,1)S(1)} %get-tuple-element.12.odd_x, bf16[1024,2048]{1,0:T(8,128)(2,1)S(1)} %get-tuple-element.13.basis, ...), custom_call_target="tpu_custom_call" | custom-call | tf_op jit(solution)/shard_map/synthesize/pallas_call | solution.py:375

commit v5 on v4

--- a/solution.py
+++ b/solution.py
@@ -188,19 +188,17 @@
     e_all[z] = energy
     pl.semaphore_wait(ring_sems.at[1], 10)
     signal(ring_sems.at[2])
-    for axes, flip in (((1, 2), 0), ((1,), 1), ((2,), 1)):
-        send_all((beside, across), axes, flip)
-    send_all((0,), (1, 2), 1)
-
     for d in range(1, 4):
         pltpu.make_async_remote_copy(
             src_ref=e_mine.at[0], dst_ref=e_all.at[z], send_sem=e_sems.at[2], recv_sem=e_sems.at[3],
             device_id={"blk": at(d, 0, 0, 0)}, device_id_type=MESH,
         ).start()
+    for axes, flip in (((1, 2), 0), ((1,), 1), ((2,), 1)):
+        send_all((beside, across), axes, flip)
+    send_all((0,), (1, 2), 1)
+
     pl.semaphore_wait(ring_sems.at[2], 10)
     send_all((beside, across), (1, 2), 1)
-    for axes, flip in (((), 0), ((2,), 0), ((1,), 0), ((), 1), ((1, 2), 0), ((1,), 1), ((2,), 1), ((1, 2), 1)):
-        send_all((2,), axes, flip)
     inbox[me] = outbox[me]
 
 
@@ -284,6 +282,8 @@
         return carry
 
     lax.fori_loop(1, PLANE, tell, 0)
+    for axes, flip in (((), 0), ((2,), 0), ((1,), 0), ((), 1), ((1, 2), 0), ((1,), 1), ((2,), 1), ((1, 2), 1)):
+        send_all((2,), axes, flip)
     lax.fori_loop(1, 3, build_first, 0)
     lax.fori_loop(0, 8, sum_first, 0)
     told = pltpu.make_async_remote_copy(

time: 47.7 us -> 47.7 us (level)
  no operation moved by 1% of the time
where the time goes in v5:
time: 47.7 us; the launch traced here: 47.6 us
  Pallas kernels  46.9 us (98%)
  between operations  0.64 us (1%)
    pallas_call x1, Pallas kernels, shards(): pl.pallas_call(exchange, out_shape=(jax.ShapeDtypeStruct((COLS, 128), BF1...  44 us
    pallas_call x1, Pallas kernels, shards(): pl.pallas_call(synthesize, out_shape=(jax.ShapeDtypeStruct((8, FIELDS, NL...  2.93 us

profile of v5, /device:TPU:1, one launch (start us, length us, event | category | flops | bytes accessed | tf_op | source)
XLA Modules:
  0.0 47.6 jit_solution(10512739562552999422)
XLA Ops:
  0.6 44.0 %exchange.1 = (bf16[512,128]{1,0:T(8,128)(2,1)S(1)}, bf16[512,128]{1,0:T(8,128)(2,1)S(1)}, bf16[1024,2048]{1,0:T(8,128)(2,1)S(1)}, f32[512,2048]{1,0:T(8,128)S(1...) custom-call(s32[2,128]{1,0:T(2,128)} %bitcast.12, s32[8,128]{1,0:T(8,128)} %bitcast.11, bf16[2049,2,128]{2,1,0:T(2,128)(2,1)} %bitcast.10, ...), custom_call_target="tpu_custom_call" | custom-call | tf_op jit(solution)/shard_map/exchange/pallas_call | solution.py:334
  44.6 2.9 %synthesize.1 = (bf16[8,64,4096]{2,1,0:T(8,128)(2,1)}, f32[1,64]{1,0:T(1,128)}) custom-call(f32[1,128]{1,0:T(1,128)S(1)} %get-tuple-element.10.energy_in, bf16[512,128]{1,0:T(8,128)(2,1)S(1)} %get-tuple-element.11.even_x, bf16[512,128]{1,0:T(8,128)(2,1)S(1)} %get-tuple-element.12.odd_x, bf16[1024,2048]{1,0:T(8,128)(2,1)S(1)} %get-tuple-element.13.basis, ...), custom_call_target="tpu_custom_call" | custom-call | tf_op jit(solution)/shard_map/synthesize/pallas_call | solution.py:375

commit v6 on v5

--- a/solution.py
+++ b/solution.py
@@ -39,8 +39,8 @@
 
 def exchange(
     orders_hbm, cycles_hbm, coef_hbm, leg_hbm,
-    even_x, odd_x, basis, evens, odds, energy_ref,
-    orders_v, cycles, coef, leg, first_x, stacked, spec, onehot, outbox, inbox, wide, order_cols, e_mine, e_plane, e_all,
+    even_x, odd_x, basis, energy_ref,
+    orders_v, cycles, coef, leg, stacked, spec, onehot, outbox, inbox, wide, order_cols, e_mine, e_plane, e_all,
     small_sems, coef_sem, leg_sem, send_sem, recv_sem, e_sems, ring_sems,
 ):
     me = lax.axis_index("blk")
@@ -162,13 +162,12 @@
 
     beside = 1 + 2 * (z % 2)
     across = 4 - beside
-    send_all((beside, 0, across), (2,), 0)
-    send_all((beside, 0, across), (1,), 0)
-    send_all((beside, 0, across), (), 1)
-    send_all((beside, across), (), 0)
-    send_all((0,), (1, 2), 0)
-    send_all((0,), (1,), 1)
-    send_all((0,), (2,), 1)
+    send_all((2, 1, 3), (), 0)
+    send_all((2, 1, 3, 0), (2,), 0)
+    send_all((2, 1, 3, 0), (1,), 0)
+    send_all((2, 1, 3, 0), (), 1)
+    for axes, flip in (((1, 2), 0), ((1,), 1), ((2,), 1)):
+        send_all((0,), axes, flip)
 
     place = me % PLANE
     is_even = lax.broadcasted_iota(I32, (1, 128), 1) < FIELDS
@@ -194,16 +193,18 @@
             device_id={"blk": at(d, 0, 0, 0)}, device_id_type=MESH,
         ).start()
     for axes, flip in (((1, 2), 0), ((1,), 1), ((2,), 1)):
-        send_all((beside, across), axes, flip)
+        send_all((2,), axes, flip)
     send_all((0,), (1, 2), 1)
-
     pl.semaphore_wait(ring_sems.at[2], 10)
-    send_all((beside, across), (1, 2), 1)
+    send_all((2,), (1, 2), 1)
+    for axes, flip in (((1, 2), 0), ((1,), 1), ((2,), 1)):
+        send_all((1, 3), axes, flip)
     inbox[me] = outbox[me]
 
 
     def back_of(slot):
-        return slot % 2 * across * (1 - slot // 2) + slot // 2 * (beside + slot % 2 * (2 - beside))
+        late = slot // 2
+        return (1 - late) * 2 * slot + late * (across + slot % 2 * (beside - across))
 
     lane = lax.broadcasted_iota(I32, (16, 128), 1)
 
@@ -253,13 +254,7 @@
         def _():
             landed(back_of(slot), PLANE)
 
-        build(slot, first_x.at[0], first_x.at[1], pl.multiple_of(slot * 128, 128))
-        return carry
-
-    def sum_first(n, carry):
-        cols = pl.ds(pl.multiple_of(n * 256, 256), 256)
-        evens[:, cols] = jnp.dot(first_x[0], basis[:384, cols], preferred_element_type=F32)
-        odds[:, cols] = jnp.dot(first_x[1], basis[COLS : COLS + 384, cols], preferred_element_type=F32)
+        build(slot, even_x, odd_x, pl.multiple_of(slot * 128, 128))
         return carry
 
     told = pltpu.make_async_remote_copy(
@@ -282,10 +277,8 @@
         return carry
 
     lax.fori_loop(1, PLANE, tell, 0)
-    for axes, flip in (((), 0), ((2,), 0), ((1,), 0), ((), 1), ((1, 2), 0), ((1,), 1), ((2,), 1), ((1, 2), 1)):
-        send_all((2,), axes, flip)
+    send_all((1, 3), (1, 2), 1)
     lax.fori_loop(1, 3, build_first, 0)
-    lax.fori_loop(0, 8, sum_first, 0)
     told = pltpu.make_async_remote_copy(
         src_ref=e_plane.at[pl.ds(0, PLANE - 1)], dst_ref=e_plane.at[pl.ds(0, PLANE - 1)],
         send_sem=e_sems.at[0], recv_sem=e_sems.at[1], device_id={"blk": at(0, 0, 0, 1)}, device_id_type=MESH,
@@ -297,8 +290,7 @@
         total = total + e_plane[s]
     energy_ref[...] = total
 
-    landed(2, PLANE)
-    build(3, even_x, odd_x, 0)
+    lax.fori_loop(3, 4, build_first, 0)
     sent = pltpu.make_async_remote_copy(
         src_ref=outbox.at[pl.ds(0, NBLK - 1)], dst_ref=inbox.at[pl.ds(0, NBLK - 1)],
         send_sem=send_sem, recv_sem=recv_sem.at[0], device_id={"blk": at(0, 0, 0, 1)}, device_id_type=MESH,
@@ -306,15 +298,15 @@
     sent.wait_send()
 
 
-def synthesize(energy_in, even_x, odd_x, basis, evens, odds, potential_hbm, energy_ref, tile, tile_sems):
+def synthesize(energy_in, even_x, odd_x, basis, potential_hbm, energy_ref, tile, tile_sems):
     both = energy_in[...]
     energy_ref[...] = (both[:, :FIELDS] + both[:, FIELDS:]) * (1.0 / NLAT)
     steps = HALF // 256
     copies = []
     for n in range(steps):
         cols = slice(n * 256, (n + 1) * 256)
-        even = evens[:, cols] + jnp.dot(even_x[...], basis[384:COLS, cols], preferred_element_type=F32)
-        odd = odds[:, cols] + jnp.dot(odd_x[...], basis[COLS + 384 :, cols], preferred_element_type=F32)
+        even = jnp.dot(even_x[...], basis[:COLS, cols], preferred_element_type=F32)
+        odd = jnp.dot(odd_x[...], basis[COLS:, cols], preferred_element_type=F32)
         for half in range(2):
             tile[n, half] = (even + odd if half == 0 else even - odd).astype(BF16).reshape(8, FIELDS, 256)
             copy = pltpu.make_async_copy(
@@ -331,24 +323,21 @@
     vmem = pl.BlockSpec(memory_space=pltpu.VMEM)
     coef = load_coef.transpose(1, 0, 2)
     table = legendre.transpose(1, 0, 2).reshape(ROWS, 2, 8, 128).transpose(0, 2, 1, 3)
-    even_x, odd_x, basis, evens, odds, energy = pl.pallas_call(
+    even_x, odd_x, basis, energy = pl.pallas_call(
         exchange,
         out_shape=(
-            jax.ShapeDtypeStruct((COLS, 128), BF16),
-            jax.ShapeDtypeStruct((COLS, 128), BF16),
+            jax.ShapeDtypeStruct((COLS, COLS), BF16),
+            jax.ShapeDtypeStruct((COLS, COLS), BF16),
             jax.ShapeDtypeStruct((2 * COLS, HALF), BF16),
-            jax.ShapeDtypeStruct((COLS, HALF), F32),
-            jax.ShapeDtypeStruct((COLS, HALF), F32),
             jax.ShapeDtypeStruct((1, 128), F32),
         ),
         in_specs=[pl.BlockSpec(memory_space=pltpu.HBM)] * 4,
-        out_specs=(vmem,) * 6,
+        out_specs=(vmem,) * 4,
         scratch_shapes=[
             pltpu.VMEM((2, 128), I32),
             pltpu.VMEM((8, 128), I32),
             pltpu.VMEM((ROWS, 2, 128), BF16),
             pltpu.VMEM((8, ROWS, 2, 128), BF16),
-            pltpu.VMEM((2, COLS, 384), BF16),
             pltpu.VMEM((COLS, 2 * ROWS), BF16),
             pltpu.VMEM((COLS, NLAT), BF16),
             pltpu.VMEM((NLAT, NLAT), BF16),
@@ -378,7 +367,7 @@
             jax.ShapeDtypeStruct((8, FIELDS, NLON), BF16),
             jax.ShapeDtypeStruct((1, FIELDS), F32),
         ),
-        in_specs=[vmem] * 6,
+        in_specs=[vmem] * 4,
         out_specs=(any_space, vmem),
         scratch_shapes=[
             pltpu.VMEM((8, 2, 8, FIELDS, 256), BF16),
@@ -386,7 +375,7 @@
         ],
         compiler_params=pltpu.CompilerParams(vmem_limit_bytes=20 * 1024 * 1024),
         name="synthesize",
-    )(energy, even_x, odd_x, basis, evens, odds)
+    )(energy, even_x, odd_x, basis)
     return potential, energy.reshape(FIELDS)
 
 

time: 47.7 us -> 46.3 us (0.971)
  the two profiles are of different devices: /device:TPU:1 before, /device:TPU:33 now
where the time goes in v6:
time: 46.3 us; the launch traced here: 46.2 us
  Pallas kernels  45.6 us (98%)
  between operations  0.64 us (1%)
    pallas_call x1, Pallas kernels, shards(): pl.pallas_call(exchange, out_shape=(jax.ShapeDtypeStruct((COLS, COLS), BF...  41.7 us
    pallas_call x1, Pallas kernels, shards(): pl.pallas_call(synthesize, out_shape=(jax.ShapeDtypeStruct((8, FIELDS, NL...  3.84 us

profile of v6, /device:TPU:33, one launch (start us, length us, event | category | flops | bytes accessed | tf_op | source)
XLA Modules:
  0.0 46.2 jit_solution(8539541587903226724)
XLA Ops:
  0.6 41.7 %exchange.1 = (bf16[512,512]{1,0:T(8,128)(2,1)S(1)}, bf16[512,512]{1,0:T(8,128)(2,1)S(1)}, bf16[1024,2048]{1,0:T(8,128)(2,1)S(1)}, f32[1,128]{1,0:T(1,128)S(1)}) custom-call(s32[2,128]{1,0:T(2,128)} %bitcast.12, s32[8,128]{1,0:T(8,128)} %bitcast.11, bf16[2049,2,128]{2,1,0:T(2,128)(2,1)} %bitcast.10, bf16[2049,8,2,128]{3,2,1,0:T(2,128)(2,1)} %bitcast.9), custom_call_target="tpu_custom_call" | custom-call | tf_op jit(solution)/shard_map/exchange/pallas_call | solution.py:326
  42.4 3.8 %synthesize.1 = (bf16[8,64,4096]{2,1,0:T(8,128)(2,1)}, f32[1,64]{1,0:T(1,128)}) custom-call(f32[1,128]{1,0:T(1,128)S(1)} %get-tuple-element.8.energy_in, bf16[512,512]{1,0:T(8,128)(2,1)S(1)} %get-tuple-element.9.even_x, bf16[512,512]{1,0:T(8,128)(2,1)S(1)} %get-tuple-element.10.odd_x, bf16[1024,2048]{1,0:T(8,128)(2,1)S(1)} %get-tuple-element.11.basis), custom_call_target="tpu_custom_call" | custom-call | tf_op jit(solution)/shard_map/synthesize/pallas_call | solution.py:364

commit v7 on v6

--- a/solution.py
+++ b/solution.py
@@ -106,34 +106,23 @@
     for copy in leg_copies[4:]:
         copy.start()
 
-    def legs(jp, carry):
-        for jt in range(2):
-            pltpu.make_async_copy(leg_hbm.at[:, 2 * jp + jt], leg.at[2 * jp + jt], leg_sem.at[2 * jp + jt]).wait()
+    for jp in range(4):
+        leg_copies[2 * jp].wait()
+        leg_copies[2 * jp + 1].wait()
         table = jnp.concatenate(
             [leg[2 * jp].reshape(2 * ROWS, 128), leg[2 * jp + 1].reshape(2 * ROWS, 128)], axis=1
         )
-        spec[:, pl.ds(pl.multiple_of(jp * 256, 256), 256)] = jnp.dot(
+        spec[:, jp * 256 : (jp + 1) * 256] = jnp.dot(
             stacked[...], table, preferred_element_type=F32
         ).astype(BF16)
-        return carry
-
-    lax.fori_loop(0, 3, legs, 0)
-    pl.semaphore_wait(ring_sems.at[0], 10)
-    signal(ring_sems.at[1])
-    lax.fori_loop(3, 4, legs, 0)
-
-    def choose(ib, carry):
-        row = pl.multiple_of(ib * 256, 256)
-        outbox[pl.ds(pl.multiple_of(ib * 32, 32), 32)] = (
-            lax.dot_general(
-                onehot[pl.ds(row, 256), :], spec[...], (((1,), (1,)), ((), ())), preferred_element_type=F32
-            )
-            .reshape(32, 8, COLS)
-            .astype(BF16)
-        )
-        return carry
-
-    lax.fori_loop(0, 4, choose, 0)
+        if jp == 2:
+            pl.semaphore_wait(ring_sems.at[0], 10)
+            signal(ring_sems.at[1])
+    outbox[...] = (
+        lax.dot_general(onehot[...], spec[...], (((1,), (1,)), ((), ())), preferred_element_type=F32)
+        .reshape(NBLK, 8, COLS)
+        .astype(BF16)
+    )
 
     def send(dz, dy, dx, dc):
         target = at(dz, dy, dx, dc)

time: 46.3 us -> 49.3 us (1.065)
  Pallas kernels: 45.6 us -> 48.6 us
    pallas_call x1, Pallas kernels: 41.7 us -> 44.8 us  [shards(): pl.pallas_call(exchange, out_shape=(jax.ShapeDtypeStruct((COLS, COLS), BF...]
where the time goes in v7:
time: 49.3 us; the launch traced here: 49.2 us
  Pallas kernels  48.6 us (99%)
  between operations  0.64 us (1%)
    pallas_call x1, Pallas kernels, shards(): pl.pallas_call(exchange, out_shape=(jax.ShapeDtypeStruct((COLS, COLS), BF...  44.8 us
    pallas_call x1, Pallas kernels, shards(): pl.pallas_call(synthesize, out_shape=(jax.ShapeDtypeStruct((8, FIELDS, NL...  3.83 us

profile of v7, /device:TPU:33, one launch (start us, length us, event | category | flops | bytes accessed | tf_op | source)
XLA Modules:
  0.0 49.2 jit_solution(14935234776602513527)
XLA Ops:
  0.6 44.8 %exchange.1 = (bf16[512,512]{1,0:T(8,128)(2,1)S(1)}, bf16[512,512]{1,0:T(8,128)(2,1)S(1)}, bf16[1024,2048]{1,0:T(8,128)(2,1)S(1)}, f32[1,128]{1,0:T(1,128)S(1)}) custom-call(s32[2,128]{1,0:T(2,128)} %bitcast.12, s32[8,128]{1,0:T(8,128)} %bitcast.11, bf16[2049,2,128]{2,1,0:T(2,128)(2,1)} %bitcast.10, bf16[2049,8,2,128]{3,2,1,0:T(2,128)(2,1)} %bitcast.9), custom_call_target="tpu_custom_call" | custom-call | tf_op jit(solution)/shard_map/exchange/pallas_call | solution.py:315
  45.4 3.8 %synthesize.1 = (bf16[8,64,4096]{2,1,0:T(8,128)(2,1)}, f32[1,64]{1,0:T(1,128)}) custom-call(f32[1,128]{1,0:T(1,128)S(1)} %get-tuple-element.8.energy_in, bf16[512,512]{1,0:T(8,128)(2,1)S(1)} %get-tuple-element.9.even_x, bf16[512,512]{1,0:T(8,128)(2,1)S(1)} %get-tuple-element.10.odd_x, bf16[1024,2048]{1,0:T(8,128)(2,1)S(1)} %get-tuple-element.11.basis), custom_call_target="tpu_custom_call" | custom-call | tf_op jit(solution)/shard_map/synthesize/pallas_call | solution.py:353

commit v8 on v6

--- a/solution.py
+++ b/solution.py
@@ -88,18 +88,26 @@
     coef_copy.wait()
     for copy in leg_copies[:4]:
         copy.start()
-    packed = coef[...].reshape(2 * ROWS, 128).T
-    column = lax.broadcasted_iota(I32, (1, 2 * ROWS), 1)
-    row_id, pair_id = column >> 1, column & 1
-    for p in range(2):
-        order = order_cols[pl.ds(me * 2 + p, 1), :][:, :1]
-        lower = jnp.where(row_id < DEGREE + 1 - order, 1, 0)
-        parity_of = jnp.where(pair_id == p, (lower + order + 1) & 1, 2)
-        for parity in range(2):
-            keep = jnp.where(parity_of == parity, 1.0, 0.0).astype(BF16)
-            for part in range(2):
-                row = ((p * 2 + part) * 2 + parity) * 64
-                stacked[row : row + 64, :] = packed[part * 64 : (part + 1) * 64] * keep
+    def stack(columns, first, count):
+        packed = coef[pl.ds(first, count)].reshape(2 * count, 128).T
+        column = lax.broadcasted_iota(I32, (1, 2 * count), 1)
+        row_id, pair_id = first + (column >> 1), column & 1
+        for p in range(2):
+            order = order_cols[pl.ds(me * 2 + p, 1), :][:, :1]
+            lower = jnp.where(row_id < DEGREE + 1 - order, 1, 0)
+            parity_of = jnp.where(pair_id == p, (lower + order + 1) & 1, 2)
+            for parity in range(2):
+                keep = jnp.where(parity_of == parity, 1.0, 0.0).astype(BF16)
+                for part in range(2):
+                    row = ((p * 2 + part) * 2 + parity) * 64
+                    stacked[row : row + 64, columns] = packed[part * 64 : (part + 1) * 64] * keep
+
+    def stack_step(k, carry):
+        stack(pl.ds(pl.multiple_of(k * 1024, 1024), 1024), k * 512, 512)
+        return carry
+
+    lax.fori_loop(0, 4, stack_step, 0)
+    stack(slice(2 * ROWS - 2, 2 * ROWS), ROWS - 1, 1)
 
     pl.semaphore_wait(barrier, 10)
     signal(ring_sems.at[0])

time: 46.3 us -> 46.2 us (level)
  no operation moved by 1% of the time
where the time goes in v8:
time: 46.2 us; the launch traced here: 46.1 us
  Pallas kernels  45.5 us (98%)
  between operations  0.64 us (1%)
    pallas_call x1, Pallas kernels, shards(): pl.pallas_call(exchange, out_shape=(jax.ShapeDtypeStruct((COLS, COLS), BF...  41.7 us
    pallas_call x1, Pallas kernels, shards(): pl.pallas_call(synthesize, out_shape=(jax.ShapeDtypeStruct((8, FIELDS, NL...  3.84 us

profile of v8, /device:TPU:33, one launch (start us, length us, event | category | flops | bytes accessed | tf_op | source)
XLA Modules:
  0.0 46.1 jit_solution(8941571816111763515)
XLA Ops:
  0.6 41.7 %exchange.1 = (bf16[512,512]{1,0:T(8,128)(2,1)S(1)}, bf16[512,512]{1,0:T(8,128)(2,1)S(1)}, bf16[1024,2048]{1,0:T(8,128)(2,1)S(1)}, f32[1,128]{1,0:T(1,128)S(1)}) custom-call(s32[2,128]{1,0:T(2,128)} %bitcast.12, s32[8,128]{1,0:T(8,128)} %bitcast.11, bf16[2049,2,128]{2,1,0:T(2,128)(2,1)} %bitcast.10, bf16[2049,8,2,128]{3,2,1,0:T(2,128)(2,1)} %bitcast.9), custom_call_target="tpu_custom_call" | custom-call | tf_op jit(solution)/shard_map/exchange/pallas_call | solution.py:334
  42.3 3.8 %synthesize.1 = (bf16[8,64,4096]{2,1,0:T(8,128)(2,1)}, f32[1,64]{1,0:T(1,128)}) custom-call(f32[1,128]{1,0:T(1,128)S(1)} %get-tuple-element.8.energy_in, bf16[512,512]{1,0:T(8,128)(2,1)S(1)} %get-tuple-element.9.even_x, bf16[512,512]{1,0:T(8,128)(2,1)S(1)} %get-tuple-element.10.odd_x, bf16[1024,2048]{1,0:T(8,128)(2,1)S(1)} %get-tuple-element.11.basis), custom_call_target="tpu_custom_call" | custom-call | tf_op jit(solution)/shard_map/synthesize/pallas_call | solution.py:372
